TPU v7x, 32 devices: a whole 2x2x4 slice. The times are simulated.
32 devices in a mesh: rows: 2 (over x), ci: 4 (over z), cj: 4 (over y, core).
Axes of the slice: x: 2, y: 2, z: 4, core: 2. Of those that a mesh axis runs over, the one named last changes fastest.
Arguments:
- matrix: float32 [512, 49152], P('rows', ('ci', 'cj')), may hold values from -585 to 585
- sample: int32 [4, 4, 512], P('ci', None, 'rows'), may hold values 0 or 1
Outputs:
- cosine: float32 [4, 12288, 4, 384], P('ci', 'rows', 'cj')
All inputs are finite; a program needn't handle non-finite values. No bound on the sum of `sample` on one device may be relied on, other than what follows from the above.
Results may differ from a plain program's by a relative error of at most 0.000054.
Values sent between devices are 32-bit elements; how exact they have to be, the bound alone decides.
A program may use at most 128 MiB of HBM per device.

v0:
```python
import jax
import jax.numpy as jnp
from jax import lax
from jax.sharding import PartitionSpec as P

QUERY = 1536


EPS = 1e-06
KEEP = 2.0


def shards(matrix, sample):
    local_squares = jnp.sum(matrix * matrix, axis=0)
    total_squares = lax.psum(local_squares, "rows")
    inverse = 1.0 / jnp.sqrt(total_squares + EPS)
    unit = matrix * inverse[None, :]
    count_ci = lax.axis_size("ci")
    count_cj = lax.axis_size("cj")
    count_rows = lax.axis_size("rows")
    row_count = matrix.shape[0]
    query_slab = QUERY // (count_ci * count_cj)
    queries = unit[:, :query_slab] * KEEP
    swapped = lax.all_to_all(unit, "cj", split_axis=0, concat_axis=1, tiled=True)
    ranged = lax.all_to_all(swapped, "rows", split_axis=1, concat_axis=0, tiled=True)
    columns = lax.all_gather(ranged, "cj", axis=0, tiled=True)
    picks = lax.dynamic_index_in_dim(sample[0], lax.axis_index("cj"), 0, keepdims=False).astype(
        jnp.float32
    )
    part_group = lax.all_gather(queries, "ci", axis=1, tiled=True) * picks[:, None]
    masked = lax.all_gather(part_group, "rows", axis=0, tiled=True)
    group_width = masked.shape[1]
    reordered = masked.reshape(count_rows, count_cj, row_count // count_cj, group_width)
    reordered = jnp.transpose(reordered, (1, 0, 2, 3)).reshape(count_rows * row_count, group_width)
    result = jnp.dot(
        jnp.transpose(columns),
        reordered,
        precision=lax.Precision.HIGHEST,
        preferred_element_type=jnp.float32,
    )
    return result[None, :, None, :]


def solution(mesh):
    in_specs = (P("rows", ("ci", "cj")), P("ci", None, "rows"))
    out_specs = P("ci", "rows", "cj", None)
    return jax.shard_map(shards, mesh=mesh, in_specs=in_specs, out_specs=out_specs, check_vma=False)
```

profile of v0, /device:TPU:0, one launch (start us, length us, event | category | flops | bytes accessed | tf_op | source)
XLA Modules:
  0.0 300.6 jit_solution(17951735130250903811)
XLA Ops:
  6.5 0.0 copy-start
  6.5 0.0 all-gather.2.cloned.1.call-start
  6.5 2.3 multiply_reduce_fusion
  8.8 0.5 copy-done
  9.4 2.4 copy.11
  11.7 9.6 %psum.7 = f32[3072]{0:T(1024)S(1)} all-reduce(f32[3072]{0:T(1024)S(1)} %multiply_reduce_fusion), channel_id=1, replica_groups=mesh['rows'=2,'ci'=4,'cj'=4] {'rows'}, use_global_device_ids=true, to_apply=%region_1.0 | all-reduce | flops 3072 | bytes 24576 | tf_op jit(solution)/shard_map/psum | solution.py:15
  21.3 2.4 broadcast_multiply_fusion
  23.7 2.4 copy.12
  26.1 40.6 %all_to_all.35 = f32[4,64,3072]{2,1,0:T(8,128)S(1)} all-to-all(f32[4,64,3072]{2,1,0:T(8,128)} %bitcast.16), channel_id=1, replica_groups=mesh['rows'=2,'ci'=4,'cj'=4] {'cj'}, dimensions={0} | all-to-all | bytes 6291456 | tf_op jit(solution)/shard_map/all_to_all | solution.py:24
  66.6 3.7 %copy.13 = f32[64,4,3072]{2,1,0:T(4,128)} copy(f32[64,4,3072]{2,0,1:T(8,128)S(1)} %bitcast.15) | data formatting | bytes 6291456 | tf_op jit(solution)/shard_map/all_to_all | solution.py:24
  70.3 5.8 %all_to_all.29 = f32[64,2,6144]{2,1,0:T(2,128)} reshape(f32[64,4,3072]{2,1,0:T(4,128)} %copy.13) | data formatting | bytes 6291456 | tf_op jit(solution)/shard_map/all_to_all | solution.py:25
  76.1 3.7 %copy.14 = f32[64,2,6144]{2,0,1:T(8,128)S(1)} copy(f32[64,2,6144]{2,1,0:T(2,128)} %all_to_all.29) | data formatting | bytes 6291456 | tf_op jit(solution)/shard_map/all_to_all | solution.py:25
  79.8 39.6 %all_to_all.36 = f32[64,2,6144]{2,0,1:T(8,128)} all-to-all(f32[64,2,6144]{2,0,1:T(8,128)S(1)} %copy.14), channel_id=1, replica_groups=mesh['rows'=2,'ci'=4,'cj'=4] {'rows'}, dimensions={1} | all-to-all | bytes 6291456 | tf_op jit(solution)/shard_map/all_to_all | solution.py:25
  119.4 0.0 all-gather.2.cloned.1.call-update
  119.5 14.5 %all_gather.10 = f32[256,384]{0,1:T(8,128)S(1)} all-gather(f32[256,96]{0,1:T(8,128)S(1)} %slice_multiply_fusion), channel_id=1, replica_groups=mesh['rows'=2,'ci'=4,'cj'=4] {'ci'}, dimensions={1}, use_global_device_ids=true | all-gather | bytes 491520 | tf_op jit(solution)/shard_map/all_gather | solution.py:30
  134.0 0.2 copy.15
  134.2 0.7 dynamic-slice_convert_fusion
  134.9 0.1 broadcast_multiply_fusion.1
  135.0 8.6 %all_gather.11 = f32[512,384]{1,0:T(8,128)S(1)} all-gather(f32[256,384]{1,0:T(8,128)S(1)} %broadcast_multiply_fusion.1), channel_id=1, replica_groups=mesh['rows'=2,'ci'=4,'cj'=4] {'rows'}, dimensions={0}, use_global_device_ids=true | all-gather | bytes 1179648 | tf_op jit(solution)/shard_map/all_gather | solution.py:31
  143.6 0.1 copy.16
  143.7 57.6 %all-gather.2.cloned.1.call-done = f32[512,6144]{1,0:T(8,128)} async-done(((f32[128,6144]{1,0:T(8,128)}), f32[512,6144]{1,0:T(8,128)}) %all-gather.2.cloned.1.call-update) | async-done | bytes 12582928 | tf_op jit(solution)/shard_map/all_gather | solution.py:26
  201.3 23.3 %convolution_bitcast_fusion = f32[1,6144,1,384]{3,1,2,0:T(8,128)S(1)} fusion(f32[512,6144]{1,0:T(8,128)} %all-gather.2.cloned.1.call-done, f32[512,384]{1,0:T(8,128)S(1)} %bitcast.17), kind=kOutput, calls=%fused_computation | convolution fusion | flops 14495514624 | bytes 22806528 | tf_op jit(solution)/shard_map/dot_general | solution.py:35
  224.6 69.2 %copy.17 = f32[1,6144,1,384]{3,2,1,0:T(1,128)} copy(f32[1,6144,1,384]{3,1,2,0:T(8,128)S(1)} %convolution_bitcast_fusion) | data formatting | bytes 18874368 | tf_op jit(solution)/shard_map/broadcast_in_dim | solution.py:41
  (2 shorter events, 0.0 us)
Async XLA Ops:
  6.5 2.8 copy-start
  6.5 194.7 %all-gather.2.cloned.1.call-start = ((), (), s32[]{:S(2)}) async-start(), calls=%async_computation.2 | async-start | bytes 15728640 | tf_op jit(solution)/shard_map/all_gather | solution.py:26
Sparse Core Ops, SparseCore 0:
  119.6 81.6 all-gather.1
where the time goes:
time: 301 us
  blocking collectives  113 us (38%)
  local copies, waits for them, and re-layouts  87.9 us (29%)
  waiting for transfers between devices  57.6 us (19%)
  matrix products  23.3 us (8%)
  between operations  13.4 us (4%)
  other arithmetic  5.48 us (2%)
    broadcast_in_dim x1, local copies, waits for them, and re-layouts, shards(): return result[None, :, None, :]  69.2 us
    all_gather x1, waiting for transfers between devices, shards(): columns = lax.all_gather(ranged, 'cj', axis=0, tiled=True)  57.6 us
    all_to_all x1, blocking collectives, shards(): lax.all_to_all(unit, 'cj', split_axis=0, concat_axis=1, tiled=True)  40.6 us
    all_to_all x1, blocking collectives, shards(): lax.all_to_all(swapped, 'rows', split_axis=1, concat_axis=0, tiled=True)  39.6 us
    dot_general x1, matrix products, shards(): jnp.dot(jnp.transpose(columns), reordered, precision=lax.Precision.HIGHES...  23.3 us
    all_gather x1, blocking collectives, shards(): lax.all_gather(queries, 'ci', axis=1, tiled=True) * picks[:, None]  14.5 us
    psum x1, blocking collectives, shards(): total_squares = lax.psum(local_squares, 'rows')  9.59 us
    all_to_all x2, local copies, waits for them, and re-layouts, shards(): lax.all_to_all(swapped, 'rows', split_axis=1, concat_axis=0, tiled=True)  9.51 us
  transfers between devices with their start and end apart: 1, of which 1 were waited for; matrix products, arithmetic and copies ran while one was open for 0% of the time, Pallas kernels for 0%

commit v1 on v0

--- a/solution.py
+++ b/solution.py
@@ -1,6 +1,10 @@
+import functools
+
 import jax
 import jax.numpy as jnp
 from jax import lax
+from jax.experimental import pallas as pl
+from jax.experimental.pallas import tpu as pltpu
 from jax.sharding import PartitionSpec as P
 
 QUERY = 1536
@@ -8,6 +12,10 @@
 
 EPS = 1e-06
 KEEP = 2.0
+
+WIDTH = 128
+AHEAD = 4
+MESH = pl.DeviceIdType.MESH
 
 
 def shards(matrix, sample):
@@ -41,7 +49,250 @@
     return result[None, :, None, :]
 
 
+def split(value):
+    high = value.astype(jnp.bfloat16)
+    low = (value - high.astype(jnp.float32)).astype(jnp.bfloat16)
+    return high, low
+
+
+def kernel(
+    count_ci, chunks, query_slab,
+    mat_ref, sample_ref, out_ref,
+    buf, xb, pa, px, qa, qx, sx, qmat, stage,
+    load_sem, y_send, y_recv, x_send, x_recv, a_send, a_recv, f_send, f_recv,
+    q_load, qx_sems, sx_sems, qa_send, qa_recv, qz_send, qz_recv, out_sem,
+):
+    x, z, cj = lax.axis_index("rows"), lax.axis_index("ci"), lax.axis_index("cj")
+    y, core = cj // 2, cj % 2
+    off = (x + y) % 2
+    rows = mat_ref.shape[0]
+    slab = chunks * WIDTH
+    group = out_ref.shape[1]
+    x_peer = (1 - x, z, cj)
+    y_peer = (x, z, (1 - y) * 2 + core)
+    twin = (x, z, y * 2 + 1 - core)
+
+    def z_peer(d):
+        return (x, (z + d) % count_ci, cj)
+
+    def remote(src, dst, send, recv, device):
+        return pltpu.make_async_remote_copy(
+            src_ref=src, dst_ref=dst, send_sem=send, recv_sem=recv,
+            device_id=device, device_id_type=MESH,
+        )
+
+    def load(c):
+        start = c * WIDTH
+        if not isinstance(c, int):
+            start = pl.multiple_of(start, WIDTH)
+        return pltpu.make_async_copy(
+            mat_ref.at[:, pl.ds(start, WIDTH)], buf.at[0, c], load_sem.at[c]
+        )
+
+    def y_copy(c):
+        return remote(buf.at[0, c], buf.at[1, c], y_send.at[c], y_recv.at[c], y_peer)
+
+    def x_copy(c):
+        return remote(buf.at[1 - off, c], xb.at[c], x_send.at[c], x_recv.at[c], x_peer)
+
+    def a_copy(c):
+        return remote(buf.at[off, c], pa.at[c], a_send.at[c], a_recv.at[c], twin)
+
+    def f_copy(c):
+        return remote(xb.at[c], px.at[c], f_send.at[c], f_recv.at[c], twin)
+
+    q_in = pltpu.make_async_copy(mat_ref.at[:, pl.ds(0, WIDTH)], qa.at[z], q_load)
+    q_in.start()
+    for c in range(chunks):
+        load(c).start()
+
+    barrier = pltpu.get_barrier_semaphore()
+    peers = [x_peer, y_peer, twin] + [z_peer(d) for d in range(1, count_ci)]
+    for peer in peers:
+        pl.semaphore_signal(barrier, inc=1, device_id=peer, device_id_type=MESH)
+    pl.semaphore_wait(barrier, len(peers))
+
+    qx_copy = remote(qa.at[z], qx.at[z], qx_sems.at[0], qx_sems.at[1], x_peer)
+    sx_copy = remote(sample_ref, sx, sx_sems.at[0], sx_sems.at[1], x_peer)
+
+    def qa_copy(d, slot):
+        return remote(qa.at[z], qa.at[slot], qa_send.at[d], qa_recv.at[d], z_peer(d))
+
+    def qz_copy(d, slot):
+        return remote(qx.at[z], qx.at[slot], qz_send.at[d], qz_recv.at[d], z_peer(d))
+
+    def send_own(c):
+        load(c).wait()
+        y_copy(c).start()
+
+        @pl.when(off == 1)
+        def _():
+            x_copy(c).start()
+
+    q_in.wait()
+    qx_copy.start()
+    for c in range(AHEAD):
+        send_own(c)
+    sx_copy.start()
+    for d in range(1, count_ci):
+        qa_copy(d, z).start()
+    qx_copy.wait_recv()
+    for d in range(1, count_ci):
+        qz_copy(d, z).start()
+
+    def relay(c):
+        y_copy(c).wait_recv()
+
+        @pl.when(off == 0)
+        def _():
+            x_copy(c).start()
+
+        a_copy(c).start()
+
+        @pl.when(c + AHEAD < chunks)
+        def _():
+            send_own(c + AHEAD)
+
+    def forward(c):
+        x_copy(c).wait_recv()
+        f_copy(c).start()
+
+    def out_copy(k, part):
+        home = core if part == 0 else 1 - core
+        start = pl.multiple_of(home * slab + k * WIDTH, WIDTH)
+        return pltpu.make_async_copy(
+            stage.at[k, part], out_ref.at[pl.ds(start, WIDTH), :], out_sem.at[k, part]
+        )
+
+    def compute(k):
+        a_copy(k).wait_recv()
+        f_copy(k).wait_recv()
+        own = jnp.concatenate([jnp.transpose(buf[off, k]), jnp.transpose(xb[k])], axis=1)
+        other = jnp.concatenate([jnp.transpose(pa[k]), jnp.transpose(px[k])], axis=1)
+        both = jnp.concatenate([own, other], axis=0)
+        squares = jnp.sum(both * both, axis=1, keepdims=True)
+        inverse = 1.0 / jnp.sqrt(squares + EPS)
+        high, low = split(both)
+        left = jnp.concatenate([high, low, high], axis=1)
+        product = jnp.dot(left, qmat[...], preferred_element_type=jnp.float32) * inverse
+        for part in range(2):
+            stage[k, part] = product[part * WIDTH:(part + 1) * WIDTH]
+            out_copy(k, part).start()
+
+    def prepare():
+        for d in range(1, count_ci):
+            slot = (z + count_ci - d) % count_ci
+            qa_copy(d, slot).wait_recv()
+            qz_copy(d, slot).wait_recv()
+        sx_copy.wait_recv()
+        inverses = []
+        for i in range(count_ci):
+            first, second = qa[i], qx[i]
+            squares = jnp.sum(first * first, axis=0, keepdims=True)
+            squares += jnp.sum(second * second, axis=0, keepdims=True)
+            inverses.append(1.0 / jnp.sqrt(squares + EPS))
+        lane = lax.broadcasted_iota(jnp.int32, (rows, WIDTH), 1)
+        for half, (pieces, picks) in enumerate(((qa, sample_ref), (qx, sx))):
+            row = picks[pl.ds(cj, 1), :].astype(jnp.float32)
+            mask = jnp.transpose(jnp.broadcast_to(row, (WIDTH, rows)))
+            tiles = [jnp.zeros((rows, WIDTH), jnp.float32)] * (group // WIDTH)
+            for i in range(count_ci):
+                value = pieces[i] * inverses[i] * KEEP * mask
+                first = i * query_slab
+                if first % WIDTH:
+                    value = pltpu.roll(value, first % WIDTH, 1)
+                for t in range(first // WIDTH, (first + query_slab - 1) // WIDTH + 1):
+                    low_lane, high_lane = first - t * WIDTH, first + query_slab - t * WIDTH
+                    tiles[t] = jnp.where((lane >= low_lane) & (lane < high_lane), value, tiles[t])
+            for t, tile in enumerate(tiles):
+                high, low = split(tile)
+                where = slice(t * WIDTH, (t + 1) * WIDTH)
+                for third, piece in enumerate((high, high, low)):
+                    base = third * 2 * rows + half * rows
+                    qmat[base:base + rows, where] = piece
+
+    lag = chunks * 5 // 12
+
+    relay(0)
+
+    @pl.loop(1, lag)
+    def _(c):
+        relay(c)
+        forward(c - 1)
+
+    prepare()
+
+    @pl.loop(lag, 2 * lag - 2)
+    def _(c):
+        relay(c)
+        forward(c - 1)
+
+        @pl.loop(0, 2)
+        def _(s):
+            compute(2 * (c - lag) + s)
+
+    @pl.loop(2 * lag - 2, chunks)
+    def _(c):
+        relay(c)
+        forward(c - 1)
+        compute(c - 2)
+
+    forward(chunks - 1)
+
+    @pl.loop(chunks - 2, chunks)
+    def _(k):
+        compute(k)
+
+    @pl.loop(0, chunks)
+    def _(c):
+        y_copy(c).wait_send()
+        x_copy(c).wait_send()
+        a_copy(c).wait_send()
+        f_copy(c).wait_send()
+        out_copy(c, 0).wait()
+        out_copy(c, 1).wait()
+
+    qx_copy.wait_send()
+    sx_copy.wait_send()
+    for d in range(1, count_ci):
+        qa_copy(d, z).wait_send()
+        qz_copy(d, z).wait_send()
+
+
+def fused(matrix, sample):
+    count_ci, count_cj = lax.axis_size("ci"), lax.axis_size("cj")
+    rows, slab = matrix.shape
+    query_slab = QUERY // (count_ci * count_cj)
+    group = query_slab * count_ci
+    chunks = slab // WIDTH
+    dma = pltpu.SemaphoreType.DMA
+    blocks = pltpu.VMEM((chunks, rows, WIDTH), jnp.float32)
+    pieces = pltpu.VMEM((count_ci, rows, WIDTH), jnp.float32)
+    result = pl.pallas_call(
+        functools.partial(kernel, count_ci, chunks, query_slab),
+        out_shape=jax.ShapeDtypeStruct((2 * slab, group), jnp.float32),
+        in_specs=[
+            pl.BlockSpec(memory_space=pl.ANY),
+            pl.BlockSpec(memory_space=pltpu.VMEM),
+        ],
+        out_specs=pl.BlockSpec(memory_space=pl.ANY),
+        scratch_shapes=[
+            pltpu.VMEM((2, chunks, rows, WIDTH), jnp.float32),
+            blocks, blocks, blocks, pieces, pieces,
+            pltpu.VMEM(sample.shape[1:], sample.dtype),
+            pltpu.VMEM((6 * rows, group), jnp.bfloat16),
+            pltpu.VMEM((chunks, 2, WIDTH, group), jnp.float32),
+        ] + [dma((chunks,))] * 9 + [dma, dma((2,)), dma((2,))] + [dma((count_ci,))] * 4
+        + [dma((chunks, 2))],
+        compiler_params=pltpu.CompilerParams(
+            collective_id=0, has_side_effects=True, vmem_limit_bytes=63 * 2**20
+        ),
+    )(matrix, sample[0])
+    return result[None, :, None, :]
+
+
 def solution(mesh):
     in_specs = (P("rows", ("ci", "cj")), P("ci", None, "rows"))
     out_specs = P("ci", "rows", "cj", None)
-    return jax.shard_map(shards, mesh=mesh, in_specs=in_specs, out_specs=out_specs, check_vma=False)
+    body = fused if mesh.shape["rows"] == 2 and mesh.shape["cj"] == 4 else shards
+    return jax.shard_map(body, mesh=mesh, in_specs=in_specs, out_specs=out_specs, check_vma=False)

time: 301 us -> 95.9 us (0.32)
  blocking collectives: 113 us -> 0 us
  Pallas kernels: 0 us -> 82.6 us
  local copies, waits for them, and re-layouts: 87.9 us -> 12.1 us
  waiting for transfers between devices: 57.6 us -> 0 us
  matrix products: 23.3 us -> 0 us
  between operations: 13.4 us -> 0.01 us
  other arithmetic: 5.48 us -> 0 us
    pallas_call x0 -> x1, Pallas kernels: none -> 82.6 us  [fused(): pl.pallas_call(functools.partial(kernel, count_ci, chunks, query_slab), o...]
    all_to_all x2 -> x0, blocking collectives: 80.2 us -> none  [the longest x1 40.6 us: shards(): lax.all_to_all(unit, 'cj', split_axis=0, concat_axis=1, tiled=True)]
    all_gather x1 -> x0, waiting for transfers between devices: 57.6 us -> none  [shards(): columns = lax.all_gather(ranged, 'cj', axis=0, tiled=True)]
    broadcast_in_dim x1, local copies, waits for them, and re-layouts: 69.2 us -> 12.1 us  [fused(): return result[None, :, None, :]]
    dot_general x1 -> x0, matrix products: 23.3 us -> none  [shards(): jnp.dot(jnp.transpose(columns), reordered, precision=lax.Precision.HIGHES...]
    all_gather x2 -> x0, blocking collectives: 23.2 us -> none  [the longest x1 14.5 us: shards(): lax.all_gather(queries, 'ci', axis=1, tiled=True) * picks[:, None]]
    all_to_all x3 -> x0, local copies, waits for them, and re-layouts: 13.2 us -> none  [the longest x2 9.51 us: shards(): lax.all_to_all(swapped, 'rows', split_axis=1, concat_axis=0, tiled=True)]
    psum x1 -> x0, blocking collectives: 9.59 us -> none  [shards(): total_squares = lax.psum(local_squares, 'rows')]
  transfers between devices with their start and end apart: 1 -> 0, of which waited for: 1 -> 0; matrix products, arithmetic and copies ran while one was open for 0% -> 0% of each run, Pallas kernels for 0% -> 0%
where the time goes in v1:
time: 95.9 us; the launch traced here: 94.6 us
  Pallas kernels  82.6 us (86%)
  local copies, waits for them, and re-layouts  12.1 us (13%)
    pallas_call x1, Pallas kernels, fused(): pl.pallas_call(functools.partial(kernel, count_ci, chunks, query_slab), o...  82.6 us
    broadcast_in_dim x1, local copies, waits for them, and re-layouts, fused(): return result[None, :, None, :]  12.1 us

profile of v1, /device:TPU:0, one launch (start us, length us, event | category | flops | bytes accessed | tf_op | source)
XLA Modules:
  0.0 94.6 jit_solution(2076230983433922158)
XLA Ops:
  0.0 82.6 %shard_map.28 = f32[6144,384]{1,0:T(8,128)} custom-call(f32[256,3072]{1,0:T(8,128)} %mat_ref.1, s32[4,256]{1,0:T(4,128)} %bitcast.3), custom_call_target="tpu_custom_call" | custom-call | tf_op jit(solution)/shard_map/pallas_call | solution.py:271
  82.6 12.1 %copy.3 = f32[1,6144,1,384]{3,2,1,0:T(1,128)} copy(f32[1,6144,1,384]{3,1,2,0:T(8,128)} %bitcast.2) | data formatting | bytes 18874368 | tf_op jit(solution)/shard_map/broadcast_in_dim | solution.py:291

commit v2 on v1

--- a/solution.py
+++ b/solution.py
@@ -58,16 +58,17 @@
 def kernel(
     count_ci, chunks, query_slab,
     mat_ref, sample_ref, out_ref,
-    buf, xb, pa, px, qa, qx, sx, qmat, stage,
+    buf, xb, pa, px, qa, qx, sx, qmat,
     load_sem, y_send, y_recv, x_send, x_recv, a_send, a_recv, f_send, f_recv,
-    q_load, qx_sems, sx_sems, qa_send, qa_recv, qz_send, qz_recv, out_sem,
+    q_load, qx_sems, sx_sems, qa_send, qa_recv, qz_send, qz_recv,
 ):
     x, z, cj = lax.axis_index("rows"), lax.axis_index("ci"), lax.axis_index("cj")
     y, core = cj // 2, cj % 2
     off = (x + y) % 2
     rows = mat_ref.shape[0]
     slab = chunks * WIDTH
-    group = out_ref.shape[1]
+    group = query_slab * count_ci
+    part_rows = rows // 2
     x_peer = (1 - x, z, cj)
     y_peer = (x, z, (1 - y) * 2 + core)
     twin = (x, z, y * 2 + 1 - core)
@@ -89,17 +90,26 @@
             mat_ref.at[:, pl.ds(start, WIDTH)], buf.at[0, c], load_sem.at[c]
         )
 
-    def y_copy(c):
-        return remote(buf.at[0, c], buf.at[1, c], y_send.at[c], y_recv.at[c], y_peer)
-
-    def x_copy(c):
-        return remote(buf.at[1 - off, c], xb.at[c], x_send.at[c], x_recv.at[c], x_peer)
+    def half(h):
+        return pl.ds(h * part_rows, part_rows)
+
+    def y_copy(c, h):
+        return remote(
+            buf.at[0, c, half(h)], buf.at[1, c, half(h)], y_send.at[c, h], y_recv.at[c, h], y_peer
+        )
+
+    def x_copy(c, h):
+        return remote(
+            buf.at[1 - off, c, half(h)], xb.at[c, half(h)], x_send.at[c, h], x_recv.at[c, h], x_peer
+        )
 
     def a_copy(c):
         return remote(buf.at[off, c], pa.at[c], a_send.at[c], a_recv.at[c], twin)
 
-    def f_copy(c):
-        return remote(xb.at[c], px.at[c], f_send.at[c], f_recv.at[c], twin)
+    def f_copy(c, h):
+        return remote(
+            xb.at[c, half(h)], px.at[c, half(h)], f_send.at[c, h], f_recv.at[c, h], twin
+        )
 
     q_in = pltpu.make_async_copy(mat_ref.at[:, pl.ds(0, WIDTH)], qa.at[z], q_load)
     q_in.start()
@@ -123,11 +133,13 @@
 
     def send_own(c):
         load(c).wait()
-        y_copy(c).start()
+        for h in range(2):
+            y_copy(c, h).start()
 
         @pl.when(off == 1)
         def _():
-            x_copy(c).start()
+            for h in range(2):
+                x_copy(c, h).start()
 
     q_in.wait()
     qx_copy.start()
@@ -136,37 +148,28 @@
     sx_copy.start()
     for d in range(1, count_ci):
         qa_copy(d, z).start()
-    qx_copy.wait_recv()
-    for d in range(1, count_ci):
-        qz_copy(d, z).start()
-
-    def relay(c):
-        y_copy(c).wait_recv()
+    def relay(c, h):
+        y_copy(c, h).wait_recv()
 
         @pl.when(off == 0)
         def _():
-            x_copy(c).start()
-
-        a_copy(c).start()
-
-        @pl.when(c + AHEAD < chunks)
-        def _():
-            send_own(c + AHEAD)
-
-    def forward(c):
-        x_copy(c).wait_recv()
-        f_copy(c).start()
-
-    def out_copy(k, part):
-        home = core if part == 0 else 1 - core
-        start = pl.multiple_of(home * slab + k * WIDTH, WIDTH)
-        return pltpu.make_async_copy(
-            stage.at[k, part], out_ref.at[pl.ds(start, WIDTH), :], out_sem.at[k, part]
-        )
+            x_copy(c, h).start()
+
+        if h == 1:
+            a_copy(c).start()
+
+            @pl.when(c + AHEAD < chunks)
+            def _():
+                send_own(c + AHEAD)
+
+    def forward(c, h):
+        x_copy(c, h).wait_recv()
+        f_copy(c, h).start()
 
     def compute(k):
         a_copy(k).wait_recv()
-        f_copy(k).wait_recv()
+        for h in range(2):
+            f_copy(k, h).wait_recv()
         own = jnp.concatenate([jnp.transpose(buf[off, k]), jnp.transpose(xb[k])], axis=1)
         other = jnp.concatenate([jnp.transpose(pa[k]), jnp.transpose(px[k])], axis=1)
         both = jnp.concatenate([own, other], axis=0)
@@ -176,10 +179,14 @@
         left = jnp.concatenate([high, low, high], axis=1)
         product = jnp.dot(left, qmat[...], preferred_element_type=jnp.float32) * inverse
         for part in range(2):
-            stage[k, part] = product[part * WIDTH:(part + 1) * WIDTH]
-            out_copy(k, part).start()
-
-    def prepare():
+            home = core if part == 0 else 1 - core
+            first = (home * slab + k * WIDTH) * (group // WIDTH)
+            for t in range(group // WIDTH):
+                out_ref[pl.ds(first + t, WIDTH, stride=group // WIDTH), :] = product[
+                    part * WIDTH:(part + 1) * WIDTH, t * WIDTH:(t + 1) * WIDTH
+                ]
+
+    def inverses_of_queries():
         for d in range(1, count_ci):
             slot = (z + count_ci - d) % count_ci
             qa_copy(d, slot).wait_recv()
@@ -191,66 +198,82 @@
             squares = jnp.sum(first * first, axis=0, keepdims=True)
             squares += jnp.sum(second * second, axis=0, keepdims=True)
             inverses.append(1.0 / jnp.sqrt(squares + EPS))
+        return inverses
+
+    def prepare(side, pieces, picks, inverses):
         lane = lax.broadcasted_iota(jnp.int32, (rows, WIDTH), 1)
-        for half, (pieces, picks) in enumerate(((qa, sample_ref), (qx, sx))):
-            row = picks[pl.ds(cj, 1), :].astype(jnp.float32)
-            mask = jnp.transpose(jnp.broadcast_to(row, (WIDTH, rows)))
-            tiles = [jnp.zeros((rows, WIDTH), jnp.float32)] * (group // WIDTH)
-            for i in range(count_ci):
-                value = pieces[i] * inverses[i] * KEEP * mask
-                first = i * query_slab
-                if first % WIDTH:
-                    value = pltpu.roll(value, first % WIDTH, 1)
-                for t in range(first // WIDTH, (first + query_slab - 1) // WIDTH + 1):
-                    low_lane, high_lane = first - t * WIDTH, first + query_slab - t * WIDTH
-                    tiles[t] = jnp.where((lane >= low_lane) & (lane < high_lane), value, tiles[t])
-            for t, tile in enumerate(tiles):
-                high, low = split(tile)
-                where = slice(t * WIDTH, (t + 1) * WIDTH)
-                for third, piece in enumerate((high, high, low)):
-                    base = third * 2 * rows + half * rows
-                    qmat[base:base + rows, where] = piece
-
-    lag = chunks * 5 // 12
-
-    relay(0)
+        row = picks[pl.ds(cj, 1), :].astype(jnp.float32)
+        mask = jnp.transpose(jnp.broadcast_to(row, (WIDTH, rows)))
+        tiles = [jnp.zeros((rows, WIDTH), jnp.float32)] * (group // WIDTH)
+        for i in range(count_ci):
+            value = pieces[i] * inverses[i] * KEEP * mask
+            first = i * query_slab
+            if first % WIDTH:
+                value = pltpu.roll(value, first % WIDTH, 1)
+            for t in range(first // WIDTH, (first + query_slab - 1) // WIDTH + 1):
+                low_lane, high_lane = first - t * WIDTH, first + query_slab - t * WIDTH
+                tiles[t] = jnp.where((lane >= low_lane) & (lane < high_lane), value, tiles[t])
+        for t, tile in enumerate(tiles):
+            high, low = split(tile)
+            where = slice(t * WIDTH, (t + 1) * WIDTH)
+            for third, piece in enumerate((high, high, low)):
+                base = third * 2 * rows + side * rows
+                qmat[base:base + rows, where] = piece
+
+    def both_halves(step, c):
+        step(c, 0)
+        step(c, 1)
+
+    relay(0, 0)
+    qx_copy.wait_recv()
+    for d in range(1, count_ci):
+        qz_copy(d, z).start()
+    relay(0, 1)
+
+    lag = chunks * 3 // 8
 
     @pl.loop(1, lag)
     def _(c):
-        relay(c)
-        forward(c - 1)
-
-    prepare()
-
-    @pl.loop(lag, 2 * lag - 2)
+        both_halves(relay, c)
+        both_halves(forward, c - 1)
+
+    relay(lag, 0)
+    inverses = inverses_of_queries()
+    relay(lag, 1)
+    both_halves(forward, lag - 1)
+    prepare(0, qa, sample_ref, inverses)
+    relay(lag + 1, 0)
+    prepare(1, qx, sx, inverses)
+    relay(lag + 1, 1)
+    both_halves(forward, lag)
+
+    @pl.loop(lag + 2, 2 * lag + 2)
     def _(c):
-        relay(c)
-        forward(c - 1)
-
-        @pl.loop(0, 2)
-        def _(s):
-            compute(2 * (c - lag) + s)
-
-    @pl.loop(2 * lag - 2, chunks)
+        k = 2 * (c - lag - 2)
+        relay(c, 0)
+        compute(k)
+        relay(c, 1)
+        both_halves(forward, c - 1)
+        compute(k + 1)
+
+    @pl.loop(2 * lag + 2, chunks)
     def _(c):
-        relay(c)
-        forward(c - 1)
+        both_halves(relay, c)
+        both_halves(forward, c - 1)
         compute(c - 2)
 
-    forward(chunks - 1)
-
-    @pl.loop(chunks - 2, chunks)
-    def _(k):
-        compute(k)
+    forward(chunks - 1, 0)
+    compute(chunks - 2)
+    forward(chunks - 1, 1)
+    compute(chunks - 1)
 
     @pl.loop(0, chunks)
     def _(c):
-        y_copy(c).wait_send()
-        x_copy(c).wait_send()
         a_copy(c).wait_send()
-        f_copy(c).wait_send()
-        out_copy(c, 0).wait()
-        out_copy(c, 1).wait()
+        for h in range(2):
+            y_copy(c, h).wait_send()
+            x_copy(c, h).wait_send()
+            f_copy(c, h).wait_send()
 
     qx_copy.wait_send()
     sx_copy.wait_send()
@@ -270,25 +293,24 @@
     pieces = pltpu.VMEM((count_ci, rows, WIDTH), jnp.float32)
     result = pl.pallas_call(
         functools.partial(kernel, count_ci, chunks, query_slab),
-        out_shape=jax.ShapeDtypeStruct((2 * slab, group), jnp.float32),
+        out_shape=pltpu.VMEM((2 * slab * group // WIDTH, WIDTH), jnp.float32),
         in_specs=[
-            pl.BlockSpec(memory_space=pl.ANY),
+            pl.BlockSpec(memory_space=pltpu.HBM),
             pl.BlockSpec(memory_space=pltpu.VMEM),
         ],
-        out_specs=pl.BlockSpec(memory_space=pl.ANY),
+        out_specs=pl.BlockSpec(memory_space=pltpu.VMEM),
         scratch_shapes=[
             pltpu.VMEM((2, chunks, rows, WIDTH), jnp.float32),
             blocks, blocks, blocks, pieces, pieces,
             pltpu.VMEM(sample.shape[1:], sample.dtype),
             pltpu.VMEM((6 * rows, group), jnp.bfloat16),
-            pltpu.VMEM((chunks, 2, WIDTH, group), jnp.float32),
-        ] + [dma((chunks,))] * 9 + [dma, dma((2,)), dma((2,))] + [dma((count_ci,))] * 4
-        + [dma((chunks, 2))],
+        ] + [dma((chunks,))] + [dma((chunks, 2))] * 4 + [dma((chunks,))] * 2
+        + [dma((chunks, 2))] * 2 + [dma, dma((2,)), dma((2,))] + [dma((count_ci,))] * 4,
         compiler_params=pltpu.CompilerParams(
-            collective_id=0, has_side_effects=True, vmem_limit_bytes=63 * 2**20
+            collective_id=0, has_side_effects=True, vmem_limit_bytes=56_000_000
         ),
     )(matrix, sample[0])
-    return result[None, :, None, :]
+    return result.reshape(1, 2 * slab, 1, group)
 
 
 def solution(mesh):

time: 95.9 us -> 87.3 us (0.910); the launches traced: 94.6 us -> 87.1 us
  local copies, waits for them, and re-layouts: 12.1 us -> 3.74 us
    broadcast_in_dim x1 -> x0, local copies, waits for them, and re-layouts: 12.1 us -> none  [fused(): return result[None, :, None, :]]
    unnamed x0 -> x1, local copies, waits for them, and re-layouts: none -> 3.74 us
where the time goes in v2:
time: 87.3 us; the launch traced here: 87.1 us
  Pallas kernels  83.4 us (96%)
  local copies, waits for them, and re-layouts  3.74 us (4%)
    pallas_call x1, Pallas kernels, fused(): pl.pallas_call(functools.partial(kernel, count_ci, chunks, query_slab), o...  83.4 us
    unnamed x1, local copies, waits for them, and re-layouts  3.74 us

profile of v2, /device:TPU:0, one launch (start us, length us, event | category | flops | bytes accessed | tf_op | source)
XLA Modules:
  0.0 87.1 jit_solution(14025323131055693156)
XLA Ops:
  0.0 83.4 %shard_map.28 = f32[18432,128]{1,0:T(8,128)S(1)} custom-call(f32[256,3072]{1,0:T(8,128)} %mat_ref.1, s32[4,256]{1,0:T(4,128)} %bitcast.3), custom_call_target="tpu_custom_call" | custom-call | tf_op jit(solution)/shard_map/pallas_call | solution.py:294
  83.4 3.7 %copy.5 = f32[1,6144,1,384]{3,2,1,0:T(1,128)} copy(f32[1,6144,1,384]{3,2,1,0:T(1,128)S(1)} %bitcast.2) | data formatting | bytes 18874368

commit v3 on v2

--- a/solution.py
+++ b/solution.py
@@ -14,7 +14,7 @@
 KEEP = 2.0
 
 WIDTH = 128
-AHEAD = 4
+AHEAD = 2
 MESH = pl.DeviceIdType.MESH
 
 

time: 87.3 us -> 87.3 us (level)
  no operation moved by 1% of the time
where the time goes in v3:
time: 87.3 us; the launch traced here: 87.1 us
  Pallas kernels  83.4 us (96%)
  local copies, waits for them, and re-layouts  3.74 us (4%)
    pallas_call x1, Pallas kernels, fused(): pl.pallas_call(functools.partial(kernel, count_ci, chunks, query_slab), o...  83.4 us
    unnamed x1, local copies, waits for them, and re-layouts  3.74 us

profile of v3, /device:TPU:0, one launch (start us, length us, event | category | flops | bytes accessed | tf_op | source)
XLA Modules:
  0.0 87.1 jit_solution(16192197746897031874)
XLA Ops:
  0.0 83.4 %shard_map.28 = f32[18432,128]{1,0:T(8,128)S(1)} custom-call(f32[256,3072]{1,0:T(8,128)} %mat_ref.1, s32[4,256]{1,0:T(4,128)} %bitcast.3), custom_call_target="tpu_custom_call" | custom-call | tf_op jit(solution)/shard_map/pallas_call | solution.py:294
  83.4 3.7 %copy.5 = f32[1,6144,1,384]{3,2,1,0:T(1,128)} copy(f32[1,6144,1,384]{3,2,1,0:T(1,128)S(1)} %bitcast.2) | data formatting | bytes 18874368
